TPU v7x, 32 devices: a whole 2x2x4 slice. The times are simulated.
32 devices in a mesh: lat: 4 (over y, x), lon: 8 (over z, core).
Axes of the slice: x: 2, y: 2, z: 4, core: 2. Of those that a mesh axis runs over, the one named last changes fastest.
Arguments:
- activations: bfloat16 [4, 16, 720, 512], P(None, 'lat', 'lon'), may hold values from -48 to 48
- upstream: bfloat16 [4, 16, 720, 512], P(None, 'lat', 'lon'), may hold values from -6 to 6
- master: float32 [512, 9, 512], P(('lat', 'lon')), may hold values from -0.09375 to 0.09375
- moment_one: float32 [512, 9, 512], P(('lat', 'lon')), may hold values from -2.5 to 2.5
- moment_two: float32 [512, 9, 512], P(('lat', 'lon')), may hold values from 0.01 to 1
Outputs:
- input_grad: bfloat16 [4, 16, 720, 512], P(None, 'lat', 'lon')
- new_weights: bfloat16 [512, 9, 512], replicated
- new_master: float32 [512, 9, 512], P(('lat', 'lon'))
- new_moment_one: float32 [512, 9, 512], P(('lat', 'lon'))
- new_moment_two: float32 [512, 9, 512], P(('lat', 'lon'))
- clipped_grad: float32 [512, 9, 512], P(('lat', 'lon'))
All inputs are finite; a program needn't handle non-finite values.
Results may differ from a plain program's by a relative error of at most 0.0049.
Values may be sent and summed in bfloat16 or wider, within the bound.
A program may use at most 128 MiB of HBM per device.

v0:
```python
import math
import jax
import jax.numpy as jnp
from jax import lax
from jax.sharding import PartitionSpec as P

CIN = 512
COUT = 512
TAPS = 9
learn_rate = 0.01
beta_one = 0.9
beta_two = 0.999
adam_eps = 1e-08
decay_rate = 0.1
step_count = 10.0
norm_eps = 1e-06


def padded(block, sides, width):
    for axis, dim in sides:
        count = lax.axis_size(axis)
        forward = [(i, i + 1) for i in range(count - 1)]
        forward.append((count - 1, 0))
        backward = [(target, source) for source, target in forward]
        low = lax.ppermute(
            lax.slice_in_dim(block, block.shape[dim] - width, None, axis=dim), axis, forward
        )
        high = lax.ppermute(lax.slice_in_dim(block, 0, width, axis=dim), axis, backward)
        block = jnp.concatenate([low, block, high], axis=dim)
    return block


def mask_poles(wide_field):
    lat_index = lax.axis_index("lat")
    lat_count = lax.axis_size("lat")
    total_rows = wide_field.shape[1]
    row_ids = lax.broadcasted_iota(jnp.int32, (1, total_rows, 1, 1), 1)
    upper = jnp.logical_and(row_ids == 0, lat_index == 0)
    lower = jnp.logical_and(row_ids == total_rows - 1, lat_index == lat_count - 1)
    return jnp.where(jnp.logical_or(upper, lower), jnp.zeros((), wide_field.dtype), wide_field)


def pull_product(grad_wide, lat_rows, lon_cols):
    batch_rows = grad_wide.shape[0]
    out_width = grad_wide.shape[3]
    windows = []
    for tap_index in range(9):
        row_off, col_off = divmod(tap_index, 3)
        windows.append(
            grad_wide[
                :, 2 - row_off : 2 - row_off + lat_rows, 2 - col_off : 2 - col_off + lon_cols, :
            ].reshape(-1, out_width)
        )

    def pull_compute(shard_piece, first_row):
        piece_width = shard_piece.shape[0]
        summed = jnp.zeros((batch_rows * lat_rows * lon_cols, piece_width), jnp.float32)
        for tap_index in range(9):
            summed = summed + lax.dot_general(
                windows[tap_index],
                shard_piece[:, tap_index, :],
                (((1,), (1,)), ((), ())),
                preferred_element_type=jnp.float32,
            )
        return summed.reshape(batch_rows, lat_rows, lon_cols, piece_width)

    return pull_compute


def input_taps(act_wide, grad_flat, lat_rows, lon_cols):

    def input_compute(first_row, row_count):
        tap_parts = []
        for tap_index in range(9):
            row_off, col_off = divmod(tap_index, 3)
            tap_slab = act_wide[
                :, row_off : row_off + lat_rows, col_off : col_off + lon_cols, :
            ].reshape(-1, row_count)
            tap_parts.append(
                lax.dot_general(
                    tap_slab,
                    grad_flat,
                    (((0,), (0,)), ((), ())),
                    preferred_element_type=jnp.float32,
                )
            )
        return jnp.stack(tap_parts, axis=1)

    return input_compute


def per_device(activations, upstream, master, moment_one, moment_two):
    lat_rows = activations.shape[1]
    lon_cols = activations.shape[2]
    grad_flat = upstream.reshape(-1, upstream.shape[3])
    act_wide = mask_poles(padded(activations, (("lat", 1), ("lon", 2)), 1))
    grad_wide = mask_poles(padded(upstream, (("lat", 1), ("lon", 2)), 1))
    producer = pull_product(grad_wide, lat_rows, lon_cols)
    term_maker = input_taps(act_wide, grad_flat, lat_rows, lon_cols)
    old_weights = master.astype(jnp.bfloat16)
    old_block = lax.all_gather(old_weights, "lon", axis=0, tiled=True)
    data_sum = producer(lax.all_gather(old_block, "lat", axis=0, tiled=True), jnp.int32(0))
    input_grad = data_sum.astype(jnp.bfloat16)
    shard_rows = master.shape[0]
    lat_block = lax.psum_scatter(
        term_maker(jnp.int32(0), lax.axis_size("lat") * (shard_rows * lax.axis_size("lon"))),
        "lat",
        scatter_dimension=0,
        tiled=True,
    )
    grad_shard = lax.psum_scatter(lat_block, "lon", scatter_dimension=0, tiled=True)
    max_norm = math.sqrt(float(CIN * TAPS * COUT))
    square_sum = lax.psum(jnp.sum(grad_shard * grad_shard), ("lat", "lon"))
    clip_factor = jnp.minimum(1.0, max_norm / (jnp.sqrt(square_sum) + norm_eps))
    grad_scaled = clip_factor * grad_shard
    new_one = beta_one * moment_one + (1.0 - beta_one) * grad_scaled
    new_two = beta_two * moment_two + (1.0 - beta_two) * grad_scaled * grad_scaled
    first_hat = new_one / (1.0 - beta_one**step_count)
    second_hat = new_two / (1.0 - beta_two**step_count)
    new_master = master - learn_rate * (
        first_hat / (jnp.sqrt(second_hat) + adam_eps) + decay_rate * master
    )
    new_half = new_master.astype(jnp.bfloat16)
    lon_block = lax.all_gather(new_half, "lon", axis=0, tiled=True)
    new_weights = lax.all_gather(lon_block, "lat", axis=0, tiled=True)
    return (input_grad, new_weights, new_master, new_one, new_two, grad_scaled)


def solution(mesh):
    in_specs = (
        P(None, "lat", "lon", None),
        P(None, "lat", "lon", None),
        P(("lat", "lon"), None, None),
        P(("lat", "lon"), None, None),
        P(("lat", "lon"), None, None),
    )
    out_specs = (
        P(None, "lat", "lon", None),
        P(),
        P(("lat", "lon"), None, None),
        P(("lat", "lon"), None, None),
        P(("lat", "lon"), None, None),
        P(("lat", "lon"), None, None),
    )
    return jax.shard_map(
        per_device, mesh=mesh, in_specs=in_specs, out_specs=out_specs, check_vma=False
    )
```

profile of v0, /device:TPU:0, one launch (start us, length us, event | category | flops | bytes accessed | tf_op | source)
XLA Modules:
  0.0 431.5 jit_solution(1120258594187733168)
XLA Ops:
  7.2 3.2 fusion.90
  11.2 3.0 collective-permute-start
  16.0 1.0 fusion.89
  17.8 1.1 collective-permute-start.4
  18.9 1.9 collective-permute-start.5
  20.8 4.6 %collective-permute-done = bf16[4,1,90,512]{3,2,1,0:T(8,128)(2,1)} collective-permute-done((bf16[4,1,90,512]{3,2,1,0:T(8,128)(2,1)}, bf16[4,1,90,512]{3,2,1,0:T(8,128)(2,1)}, u32[]{:S(2)}, u32[]{:S(2)}) %collective-permute-start) | collective-permute-done | bytes 368672 | tf_op jit(solution)/shard_map/ppermute | solution.py:25
  25.4 1.0 constant_dynamic-update-slice_fusion.2
  26.8 7.6 %collective-permute-done.1 = bf16[4,1,90,512]{3,2,1,0:T(8,128)(2,1)} collective-permute-done((bf16[4,1,90,512]{3,2,1,0:T(8,128)(2,1)}, bf16[4,1,90,512]{3,2,1,0:T(8,128)(2,1)}, u32[]{:S(2)}, u32[]{:S(2)}) %collective-permute-start.1) | collective-permute-done | bytes 368672 | tf_op jit(solution)/shard_map/ppermute | solution.py:28
  34.4 1.0 constant_dynamic-update-slice_fusion
  35.6 3.5 collective-permute-start.3
  39.1 3.2 collective-permute-done.4
  42.3 1.0 constant_dynamic-update-slice_fusion.5
  43.7 6.5 %collective-permute-done.5 = bf16[4,1,90,512]{3,2,1,0:T(8,128)(2,1)} collective-permute-done((bf16[4,1,90,512]{3,2,1,0:T(8,128)(2,1)S(1)}, bf16[4,1,90,512]{3,2,1,0:T(8,128)(2,1)}, u32[]{:S(2)}, u32[]{:S(2)}) %collective-permute-start.5) | collective-permute-done | bytes 368672 | tf_op jit(solution)/shard_map/ppermute | solution.py:28
  50.1 1.0 constant_dynamic-update-slice_fusion.3
  51.3 3.5 collective-permute-start.7
  54.9 1.8 collective-permute-done.6
  56.7 2.7 maximum_select_fusion.1
  59.3 2.0 fusion.22
  61.3 2.0 fusion.28
  63.3 2.0 fusion.34
  65.4 2.0 fusion.40
  67.4 2.1 fusion.46
  69.4 2.0 fusion.52
  71.5 2.0 fusion.58
  73.4 2.1 fusion.64
  75.5 2.0 fusion.70
  77.7 95.2 %reduce-scatter.3.cloned.1.call-done = f32[128,9,512]{2,0,1:T(8,128)} async-done(((f32[512,9,512]{2,0,1:T(8,128)}), f32[128,9,512]{2,0,1:T(8,128)}) %reduce-scatter.3.cloned.1.call-update) | async-done | bytes 2359312 | tf_op jit(solution)/shard_map/reduce_scatter | solution.py:105
  173.0 39.4 %reduce-scatter.5.cloned.1.call-done = f32[16,9,512]{2,0,1:T(8,128)} async-done(((f32[128,9,512]{2,0,1:T(8,128)}), f32[16,9,512]{2,0,1:T(8,128)}) %reduce-scatter.5.cloned.1.call-update) | async-done | bytes 294928 | tf_op jit(solution)/shard_map/reduce_scatter | solution.py:111
  212.3 1.6 multiply_reduce_fusion
  214.0 37.9 %psum.7 = f32[]{:T(128)} all-reduce(f32[]{:T(128)} %multiply_reduce_fusion), channel_id=1, replica_groups=mesh['lat'=4,'lon'=8] {'lat','lon'}, use_global_device_ids=true, to_apply=%region_3.4 | all-reduce | flops 1 | bytes 8 | tf_op jit(solution)/shard_map/psum | solution.py:113
  252.6 2.2 fusion.84
  255.4 23.0 %all-gather.5.cloned.1.call-done = bf16[128,9,512]{2,0,1:T(8,128)(2,1)} async-done(((bf16[16,9,512]{2,0,1:T(8,128)(2,1)}), bf16[128,9,512]{2,0,1:T(8,128)(2,1)}) %all-gather.5.cloned.1.call-update) | async-done | bytes 1179664 | tf_op jit(solution)/shard_map/all_gather | solution.py:101
  278.7 24.2 %all-gather.9.cloned.1.call-done = bf16[128,9,512]{2,0,1:T(8,128)(2,1)} async-done(((bf16[16,9,512]{2,0,1:T(8,128)(2,1)}), bf16[128,9,512]{2,0,1:T(8,128)(2,1)}) %all-gather.9.cloned.1.call-update) | async-done | bytes 1179664 | tf_op jit(solution)/shard_map/all_gather | solution.py:124
  302.9 6.2 %fusion.87 = (bf16[4,4,90,512]{3,2,1,0:T(8,128)(2,1)}, bf16[4,4,90,512]{3,2,1,0:T(8,128)(2,1)}, bf16[4,4,90,512]{3,2,1,0:T(8,128)(2,1)}, bf16[4,4,90,512]{3,2,1,...) fusion(bf16[4,6,92,512]{3,2,1,0:T(8,128)(2,1)S(1)} %get-tuple-e, ...), kind=kLoop, calls=%fused_computation.81 | loop fusion | bytes 26542080 | tf_op jit(solution)/shard_map/slice | solution.py:50
  309.1 1.7 reshape.66
  310.9 2.7 reshape.67
  313.5 1.4 reshape.68
  314.9 2.6 reshape.69
  317.5 2.4 reshape.70
  319.9 1.3 reshape.71
  321.2 2.6 reshape.72
  323.8 2.5 reshape.73
  326.3 1.3 reshape.74
  327.6 33.6 %all-gather.7.cloned.1.call-done = bf16[512,9,512]{2,0,1:T(8,128)(2,1)} async-done(((bf16[128,9,512]{2,0,1:T(8,128)(2,1)}), bf16[512,9,512]{2,0,1:T(8,128)(2,1)}) %all-gather.7.cloned.1.call-update) | async-done | bytes 4718608 | tf_op jit(solution)/shard_map/all_gather | solution.py:102
  361.2 2.2 fusion.73
  375.2 2.3 copy.42
  377.4 42.5 %all-gather.11.cloned.1.call-done = bf16[512,9,512]{2,0,1:T(8,128)(2,1)} async-done(((bf16[128,9,512]{2,0,1:T(8,128)(2,1)}), bf16[512,9,512]{2,0,1:T(8,128)(2,1)}) %all-gather.11.cloned.1.call-update) | async-done | bytes 4718608 | tf_op jit(solution)/shard_map/all_gather | solution.py:125
  419.9 4.8 %copy.89 = bf16[512,9,512]{2,0,1:T(8,128)(2,1)} copy(bf16[512,9,512]{2,0,1:T(8,128)(2,1)} %all-gather.11.cloned.1.call-done) | data formatting | bytes 9437184
  (72 shorter events, 17.2 us)
Async XLA Ops:
  7.2 8.8 %copy-start.3 = (bf16[4,4,90,512]{3,1,2,0:T(4,128)(2,1)S(1)}, bf16[4,4,90,512]{3,1,2,0:T(4,128)(2,1)}, u32[]{:S(2)}) copy-start(bf16[4,4,90,512]{3,1,2,0:T(4,128)(2,1)} %param.5) | copy-start | bytes 4423684
  7.2 165.7 %reduce-scatter.3.cloned.1.call-start = ((), (), s32[]{:S(2)}) async-start(), calls=%async_computation.4 | async-start | bytes 11796480 | tf_op jit(solution)/shard_map/reduce_scatter | solution.py:105
  11.2 14.2 %collective-permute-start = (bf16[4,1,90,512]{3,2,1,0:T(8,128)(2,1)}, bf16[4,1,90,512]{3,2,1,0:T(8,128)(2,1)}, u32[]{:S(2)}, u32[]{:S(2)}) collective-permute-start(bf16[4,1,90,512]{3,2,1,0:T(8,128)(2,1)} %copy.72), channel_id=1, source_target_pairs={{0,8},{8,16},{16,24},{24,0},{1,9},{9,17},{17,25},{25,1},{2,10},{10... | collective-permute-start | bytes 1105928 | tf_op jit(solution)/shard_map/ppermute | solution.py:25
  15.0 11.5 %copy-start.4 = (bf16[4,4,90,512]{3,1,2,0:T(4,128)(2,1)S(1)}, bf16[4,4,90,512]{3,1,2,0:T(4,128)(2,1)}, u32[]{:S(2)}) copy-start(bf16[4,4,90,512]{3,1,2,0:T(4,128)(2,1)} %param.6) | copy-start | bytes 4423684
  15.0 19.4 %collective-permute-start.1 = (bf16[4,1,90,512]{3,2,1,0:T(8,128)(2,1)}, bf16[4,1,90,512]{3,2,1,0:T(8,128)(2,1)}, u32[]{:S(2)}, u32[]{:S(2)}) collective-permute-start(bf16[4,1,90,512]{3,2,1,0:T(8,128)(2,1)} %copy.73), channel_id=1, source_target_pairs={{8,0},{16,8},{24,16},{0,24},{9,1},{17,9},{25,17},{1,25},{10,2},{18... | collective-permute-start | bytes 1105928 | tf_op jit(solution)/shard_map/ppermute | solution.py:28
  17.8 24.5 %collective-permute-start.4 = (bf16[4,1,90,512]{3,2,1,0:T(8,128)(2,1)}, bf16[4,1,90,512]{3,2,1,0:T(8,128)(2,1)}, u32[]{:S(2)}, u32[]{:S(2)}) collective-permute-start(bf16[4,1,90,512]{3,2,1,0:T(8,128)(2,1)} %copy.74), channel_id=1, source_target_pairs={{0,8},{8,16},{16,24},{24,0},{1,9},{9,17},{17,25},{25,1},{2,10},{10... | collective-permute-start | bytes 1105928 | tf_op jit(solution)/shard_map/ppermute | solution.py:25
  18.9 31.2 %collective-permute-start.5 = (bf16[4,1,90,512]{3,2,1,0:T(8,128)(2,1)S(1)}, bf16[4,1,90,512]{3,2,1,0:T(8,128)(2,1)}, u32[]{:S(2)}, u32[]{:S(2)}) collective-permute-start(bf16[4,1,90,512]{3,2,1,0:T(8,128)(2,1)S(1)} %copy.75), channel_id=1, source_target_pairs={{8,0},{16,8},{24,16},{0,24},{9,1},{17,9},{25,17},{1,25},{10,2},{18... | collective-permute-start | bytes 1105928 | tf_op jit(solution)/shard_map/ppermute | solution.py:28
  35.5 19.3 %collective-permute-start.2 = (bf16[4,6,1,512]{3,2,1,0:T(2,128)(2,1)S(1)}, bf16[4,6,1,512]{3,2,1,0:T(2,128)(2,1)S(1)}, u32[]{:S(2)}, u32[]{:S(2)}) collective-permute-start(bf16[4,6,1,512]{3,2,1,0:T(2,128)(2,1)S(1)} %get-tuple-element.34), channel_id=1, source_target_pairs={{0,1},{1,2},{2,3},{3,4},{4,5},{5,6},{6,7},{7,0},{8,9},{9,10},{10,1... | collective-permute-start | bytes 73736 | tf_op jit(solution)/shard_map/ppermute | solution.py:25
  35.6 19.3 %collective-permute-start.3 = (bf16[4,6,1,512]{3,2,1,0:T(2,128)(2,1)S(1)}, bf16[4,6,1,512]{3,2,1,0:T(2,128)(2,1)S(1)}, u32[]{:S(2)}, u32[]{:S(2)}) collective-permute-start(bf16[4,6,1,512]{3,2,1,0:T(2,128)(2,1)S(1)} %get-tuple-element.35), channel_id=1, source_target_pairs={{1,0},{2,1},{3,2},{4,3},{5,4},{6,5},{7,6},{0,7},{9,8},{10,9},{11,1... | collective-permute-start | bytes 73736 | tf_op jit(solution)/shard_map/ppermute | solution.py:28
  51.2 5.4 %collective-permute-start.6 = (bf16[4,6,1,512]{3,2,1,0:T(2,128)(2,1)S(1)}, bf16[4,6,1,512]{3,2,1,0:T(2,128)(2,1)S(1)}, u32[]{:S(2)}, u32[]{:S(2)}) collective-permute-start(bf16[4,6,1,512]{3,2,1,0:T(2,128)(2,1)S(1)} %get-tuple-element.23), channel_id=1, source_target_pairs={{0,1},{1,2},{2,3},{3,4},{4,5},{5,6},{6,7},{7,0},{8,9},{9,10},{10,1... | collective-permute-start | bytes 73736 | tf_op jit(solution)/shard_map/ppermute | solution.py:25
  51.3 5.3 %collective-permute-start.7 = (bf16[4,6,1,512]{3,2,1,0:T(2,128)(2,1)S(1)}, bf16[4,6,1,512]{3,2,1,0:T(2,128)(2,1)S(1)}, u32[]{:S(2)}, u32[]{:S(2)}) collective-permute-start(bf16[4,6,1,512]{3,2,1,0:T(2,128)(2,1)S(1)} %get-tuple-element.24), channel_id=1, source_target_pairs={{1,0},{2,1},{3,2},{4,3},{5,4},{6,5},{7,6},{0,7},{9,8},{10,9},{11,1... | collective-permute-start | bytes 73736 | tf_op jit(solution)/shard_map/ppermute | solution.py:28
  54.8 4.5 %copy-start.5 = (bf16[4,4,90,512]{3,1,2,0:T(4,128)(2,1)S(1)}, bf16[4,4,90,512]{3,1,2,0:T(4,128)(2,1)}, u32[]{:S(2)}) copy-start(bf16[4,4,90,512]{3,1,2,0:T(4,128)(2,1)} %param.6) | copy-start | bytes 4423684
  77.6 175.0 %copy-start.15 = (f32[16,9,512]{2,0,1:T(8,128)S(1)}, f32[16,9,512]{2,0,1:T(8,128)}, u32[]{:S(2)}) copy-start(f32[16,9,512]{2,0,1:T(8,128)} %param.7) | copy-start | bytes 884740
  77.6 175.0 %copy-start.16 = (f32[16,9,512]{2,0,1:T(8,128)S(1)}, f32[16,9,512]{2,0,1:T(8,128)}, u32[]{:S(2)}) copy-start(f32[16,9,512]{2,0,1:T(8,128)} %param.8) | copy-start | bytes 884740
  77.6 175.0 %copy-start.17 = (f32[16,9,512]{2,0,1:T(8,128)S(1)}, f32[16,9,512]{2,0,1:T(8,128)}, u32[]{:S(2)}) copy-start(f32[16,9,512]{2,0,1:T(8,128)} %param.9) | copy-start | bytes 884740
  77.6 134.7 %reduce-scatter.5.cloned.1.call-start = ((), (), s32[]{:S(2)}) async-start(), calls=%async_computation.5 | async-start | bytes 2654208 | tf_op jit(solution)/shard_map/reduce_scatter | solution.py:111
  172.9 105.5 %all-gather.5.cloned.1.call-start = ((), (), s32[]{:S(2)}) async-start(), calls=%async_computation.2 | async-start | bytes 1327104 | tf_op jit(solution)/shard_map/all_gather | solution.py:101
  254.8 48.1 %all-gather.9.cloned.1.call-start = ((), (), s32[]{:S(2)}) async-start(), calls=%async_computation.6 | async-start | bytes 1327104 | tf_op jit(solution)/shard_map/all_gather | solution.py:124
  255.4 105.8 %all-gather.7.cloned.1.call-start = ((), (), s32[]{:S(2)}) async-start(), calls=%async_computation.3 | async-start | bytes 5898240 | tf_op jit(solution)/shard_map/all_gather | solution.py:102
  278.4 141.5 %all-gather.11.cloned.1.call-start = ((), (), s32[]{:S(2)}) async-start(), calls=%async_computation.7 | async-start | bytes 5898240 | tf_op jit(solution)/shard_map/all_gather | solution.py:125
  309.1 4.4 %copy-start.2 = (bf16[4,4,90,512]{3,2,1,0:T(8,128)(2,1)S(1)}, bf16[4,4,90,512]{3,2,1,0:T(8,128)(2,1)}, u32[]{:S(2)}) copy-start(bf16[4,4,90,512]{3,2,1,0:T(8,128)(2,1)} %get-tuple-element.31) | copy-start | bytes 4423684
  314.9 5.0 %copy-start.1 = (bf16[4,4,90,512]{3,2,1,0:T(8,128)(2,1)S(1)}, bf16[4,4,90,512]{3,2,1,0:T(8,128)(2,1)}, u32[]{:S(2)}) copy-start(bf16[4,4,90,512]{3,2,1,0:T(8,128)(2,1)} %get-tuple-element.28) | copy-start | bytes 4423684
  321.2 5.1 %copy-start = (bf16[4,4,90,512]{3,2,1,0:T(8,128)(2,1)S(1)}, bf16[4,4,90,512]{3,2,1,0:T(8,128)(2,1)}, u32[]{:S(2)}) copy-start(bf16[4,4,90,512]{3,2,1,0:T(8,128)(2,1)} %get-tuple-element.25) | copy-start | bytes 4423684
  327.6 35.8 %copy-start.13 = (bf16[1440,512]{1,0:T(8,128)(2,1)S(1)}, bf16[1440,512]{1,0:T(8,128)(2,1)}, u32[]{:S(2)}) copy-start(bf16[1440,512]{1,0:T(8,128)(2,1)} %reshape.67) | copy-start | bytes 4423684
  361.2 2.5 copy-start.14
  363.7 1.4 copy-start.12
  365.1 1.4 copy-start.11
  366.5 1.4 copy-start.10
  367.8 1.4 copy-start.9
  369.2 1.6 copy-start.8
  370.8 1.5 copy-start.7
  372.3 1.5 copy-start.6
Sparse Core Ops, SparseCore 0:
  77.7 95.1 reduce-scatter.2
  175.2 37.0 reduce-scatter.4
  254.9 23.4 all-gather.4
  280.4 22.4 all-gather.8
  304.6 56.5 all-gather.6
  362.9 56.9 all-gather.10
where the time goes:
time: 432 us
  waiting for transfers between devices  282 us (65%)
  local copies, waits for them, and re-layouts  47.3 us (11%)
  blocking collectives  37.9 us (9%)
  matrix products  28.2 us (7%)
  between operations  15.1 us (3%)
  starting transfers between devices  14.5 us (3%)
  other arithmetic  6.48 us (2%)
    reduce_scatter x1, waiting for transfers between devices, per_device(): lax.psum_scatter(term_maker(jnp.int32(0), lax.axis_size('lat') * (shard_r...  95.2 us
    all_gather x1, waiting for transfers between devices, per_device(): new_weights = lax.all_gather(lon_block, 'lat', axis=0, tiled=True)  42.5 us
    reduce_scatter x1, waiting for transfers between devices, per_device(): lax.psum_scatter(lat_block, 'lon', scatter_dimension=0, tiled=True)  39.4 us
    psum x1, blocking collectives, per_device(): square_sum = lax.psum(jnp.sum(grad_shard * grad_shard), ('lat', 'lon'))  37.9 us
    all_gather x1, waiting for transfers between devices, per_device(): lax.all_gather(old_block, 'lat', axis=0, tiled=True)  33.6 us
    all_gather x1, waiting for transfers between devices, per_device(): lon_block = lax.all_gather(new_half, 'lon', axis=0, tiled=True)  24.2 us
    all_gather x1, waiting for transfers between devices, per_device(): old_block = lax.all_gather(old_weights, 'lon', axis=0, tiled=True)  23 us
    reshape x9, local copies, waits for them, and re-layouts, pull_product(): windows.append(grad_wide[:, 2 - row_off:2 - row_off + lat_rows, 2 - col_o...  18.5 us
  transfers between devices with their start and end apart: 14, of which 11 were waited for; matrix products, arithmetic and copies ran while one was open for 10% of the time, Pallas kernels for 0%

commit v1 on v0

--- a/solution.py
+++ b/solution.py
@@ -1,3 +1,4 @@
+import functools
 import math
 import jax
 import jax.numpy as jnp
@@ -14,6 +15,24 @@
 decay_rate = 0.1
 step_count = 10.0
 norm_eps = 1e-06
+
+
+def _process_spots(tile_in, comm_axis, where_dim):
+    p_count = lax.axis_size(comm_axis)
+    copies = []
+    for i0 in range(p_count):
+        copies.append((i0, (i0 + 1) % p_count))
+    h_now = [None] * p_count
+    h_now[p_count - 1] = tile_in
+    for t in range(p_count - 2, -1, -1):
+        h_now[t] = lax.ppermute(h_now[t + 1], comm_axis, copies)
+    block_next = jnp.concatenate(h_now, axis=where_dim)
+    return jnp.roll(
+        block_next, shift=(lax.axis_index(comm_axis) + 1) * tile_in.shape[where_dim], axis=where_dim
+    )
+
+
+_direct_stacks_all = functools.partial(_process_spots, comm_axis="lon", where_dim=0)
 
 
 def padded(block, sides, width):
@@ -121,7 +140,7 @@
         first_hat / (jnp.sqrt(second_hat) + adam_eps) + decay_rate * master
     )
     new_half = new_master.astype(jnp.bfloat16)
-    lon_block = lax.all_gather(new_half, "lon", axis=0, tiled=True)
+    lon_block = _direct_stacks_all(new_half)
     new_weights = lax.all_gather(lon_block, "lat", axis=0, tiled=True)
     return (input_grad, new_weights, new_master, new_one, new_two, grad_scaled)
 

time: 432 us -> 468 us (1.083)
  waiting for transfers between devices: 282 us -> 321 us
    ppermute x0 -> x7, waiting for transfers between devices: none -> 44.2 us  [_process_spots(): h_now[t] = lax.ppermute(h_now[t + 1], comm_axis, copies)]
    all_gather x1, waiting for transfers between devices: 33.6 us -> 58.7 us  [per_device(): lax.all_gather(old_block, 'lat', axis=0, tiled=True)]
    all_gather x1 -> x0, waiting for transfers between devices: 24.2 us -> none  [per_device(): lon_block = lax.all_gather(new_half, 'lon', axis=0, tiled=True)]
    ppermute x4, waiting for transfers between devices: 14.1 us -> 23.3 us  [padded(): lax.ppermute(lax.slice_in_dim(block, 0, width, axis=dim), axis, backward)]
    all_gather x1, waiting for transfers between devices: 23 us -> 16.4 us  [per_device(): old_block = lax.all_gather(old_weights, 'lon', axis=0, tiled=True)]
    all_gather x1, waiting for transfers between devices: 42.5 us -> 36.1 us  [per_device(): new_weights = lax.all_gather(lon_block, 'lat', axis=0, tiled=True)]
    unnamed x46 -> x65, local copies, waits for them, and re-layouts: 15.8 us -> 15.6 us
  transfers between devices with their start and end apart: 14 -> 20, of which waited for: 11 -> 15; matrix products, arithmetic and copies ran while one was open for 10% -> 7% of each run, Pallas kernels for 0% -> 0%
where the time goes in v1:
time: 468 us; the launch traced here: 467 us
  waiting for transfers between devices  321 us (69%)
  local copies, waits for them, and re-layouts  45.7 us (10%)
  blocking collectives  38 us (8%)
  matrix products  28.1 us (6%)
  between operations  15 us (3%)
  starting transfers between devices  13.6 us (3%)
  other arithmetic  6.43 us (1%)
    reduce_scatter x1, waiting for transfers between devices, per_device(): lax.psum_scatter(term_maker(jnp.int32(0), lax.axis_size('lat') * (shard_r...  95 us
    all_gather x1, waiting for transfers between devices, per_device(): lax.all_gather(old_block, 'lat', axis=0, tiled=True)  58.7 us
    ppermute x7, waiting for transfers between devices, _process_spots(): h_now[t] = lax.ppermute(h_now[t + 1], comm_axis, copies)  44.2 us
    reduce_scatter x1, waiting for transfers between devices, per_device(): lax.psum_scatter(lat_block, 'lon', scatter_dimension=0, tiled=True)  39.3 us
    psum x1, blocking collectives, per_device(): square_sum = lax.psum(jnp.sum(grad_shard * grad_shard), ('lat', 'lon'))  38 us
    all_gather x1, waiting for transfers between devices, per_device(): new_weights = lax.all_gather(lon_block, 'lat', axis=0, tiled=True)  36.1 us
    ppermute x4, waiting for transfers between devices, padded(): lax.ppermute(lax.slice_in_dim(block, 0, width, axis=dim), axis, backward)  23.3 us
    dot_general x9, matrix products, input_compute(): lax.dot_general(tap_slab, grad_flat, (((0,), (0,)), ((), ())), preferred_...  18.2 us
  transfers between devices with their start and end apart: 20, of which 15 were waited for; matrix products, arithmetic and copies ran while one was open for 7% of the time, Pallas kernels for 0%

profile of v1, /device:TPU:0, one launch (start us, length us, event | category | flops | bytes accessed | tf_op | source)
XLA Modules:
  0.0 467.4 jit_solution(14868597112934487830)
XLA Ops:
  7.2 3.2 fusion.90
  11.2 3.0 collective-permute-start
  16.1 1.5 collective-permute-start.4
  17.6 1.5 collective-permute-start.5
  20.0 5.5 %collective-permute-done = bf16[4,1,90,512]{3,2,1,0:T(8,128)(2,1)} collective-permute-done((bf16[4,1,90,512]{3,2,1,0:T(8,128)(2,1)}, bf16[4,1,90,512]{3,2,1,0:T(8,128)(2,1)}, u32[]{:S(2)}, u32[]{:S(2)}) %collective-permute-start) | collective-permute-done | bytes 368672 | tf_op jit(solution)/shard_map/ppermute | solution.py:44
  26.8 23.3 %collective-permute-done.1 = bf16[4,1,90,512]{3,2,1,0:T(8,128)(2,1)} collective-permute-done((bf16[4,1,90,512]{3,2,1,0:T(8,128)(2,1)}, bf16[4,1,90,512]{3,2,1,0:T(8,128)(2,1)}, u32[]{:S(2)}, u32[]{:S(2)}) %collective-permute-start.1) | collective-permute-done | bytes 368672 | tf_op jit(solution)/shard_map/ppermute | solution.py:47
  51.3 3.5 collective-permute-start.3
  56.2 1.0 constant_dynamic-update-slice_fusion.3
  57.4 3.5 collective-permute-start.7
  60.9 2.0 collective-permute-done.6
  62.9 2.7 maximum_select_fusion.1
  65.6 2.0 fusion.22
  67.6 2.0 fusion.28
  69.6 2.0 fusion.34
  71.7 2.0 fusion.40
  73.6 2.0 fusion.46
  75.7 2.0 fusion.52
  77.7 2.0 fusion.58
  79.7 2.1 fusion.64
  81.8 2.0 fusion.70
  83.9 95.0 %reduce-scatter.3.cloned.1.call-done = f32[128,9,512]{2,0,1:T(8,128)} async-done(((f32[512,9,512]{2,0,1:T(8,128)}), f32[128,9,512]{2,0,1:T(8,128)}) %reduce-scatter.3.cloned.1.call-update) | async-done | bytes 2359312 | tf_op jit(solution)/shard_map/reduce_scatter | solution.py:124
  179.0 39.3 %reduce-scatter.5.cloned.1.call-done = f32[16,9,512]{2,0,1:T(8,128)} async-done(((f32[128,9,512]{2,0,1:T(8,128)}), f32[16,9,512]{2,0,1:T(8,128)}) %reduce-scatter.5.cloned.1.call-update) | async-done | bytes 294928 | tf_op jit(solution)/shard_map/reduce_scatter | solution.py:130
  218.3 1.6 multiply_reduce_fusion
  219.9 38.0 %psum.7 = f32[]{:T(128)} all-reduce(f32[]{:T(128)} %multiply_reduce_fusion), channel_id=1, replica_groups=mesh['lat'=4,'lon'=8] {'lat','lon'}, use_global_device_ids=true, to_apply=%region_3.4 | all-reduce | flops 1 | bytes 8 | tf_op jit(solution)/shard_map/psum | solution.py:132
  258.7 2.1 fusion.84
  260.8 6.4 %collective-permute-done.8 = bf16[16,9,512]{2,0,1:T(8,128)(2,1)S(1)} collective-permute-done((bf16[16,9,512]{2,0,1:T(8,128)(2,1)S(1)}, bf16[16,9,512]{2,0,1:T(8,128)(2,1)S(1)}, u32[]{:S(2)}, u32[]{:S(2)}) %collective-permute-start.8) | collective-permute-done | bytes 147488 | tf_op jit(solution)/shard_map/ppermute | solution.py:28
  267.2 6.4 %collective-permute-done.9 = bf16[16,9,512]{2,0,1:T(8,128)(2,1)S(1)} collective-permute-done((bf16[16,9,512]{2,0,1:T(8,128)(2,1)S(1)}, bf16[16,9,512]{2,0,1:T(8,128)(2,1)S(1)}, u32[]{:S(2)}, u32[]{:S(2)}) %collective-permute-start.9) | collective-permute-done | bytes 147488 | tf_op jit(solution)/shard_map/ppermute | solution.py:28
  273.5 6.4 %collective-permute-done.10 = bf16[16,9,512]{2,0,1:T(8,128)(2,1)S(1)} collective-permute-done((bf16[16,9,512]{2,0,1:T(8,128)(2,1)S(1)}, bf16[16,9,512]{2,0,1:T(8,128)(2,1)S(1)}, u32[]{:S(2)}, u32[]{:S(2)}) %collective-permute-start.10) | collective-permute-done | bytes 147488 | tf_op jit(solution)/shard_map/ppermute | solution.py:28
  279.9 6.4 %collective-permute-done.11 = bf16[16,9,512]{2,0,1:T(8,128)(2,1)S(1)} collective-permute-done((bf16[16,9,512]{2,0,1:T(8,128)(2,1)S(1)}, bf16[16,9,512]{2,0,1:T(8,128)(2,1)S(1)}, u32[]{:S(2)}, u32[]{:S(2)}) %collective-permute-start.11) | collective-permute-done | bytes 147488 | tf_op jit(solution)/shard_map/ppermute | solution.py:28
  286.3 6.4 %collective-permute-done.12 = bf16[16,9,512]{2,0,1:T(8,128)(2,1)S(1)} collective-permute-done((bf16[16,9,512]{2,0,1:T(8,128)(2,1)S(1)}, bf16[16,9,512]{2,0,1:T(8,128)(2,1)S(1)}, u32[]{:S(2)}, u32[]{:S(2)}) %collective-permute-start.12) | collective-permute-done | bytes 147488 | tf_op jit(solution)/shard_map/ppermute | solution.py:28
  292.6 6.4 %collective-permute-done.13 = bf16[16,9,512]{2,0,1:T(8,128)(2,1)S(1)} collective-permute-done((bf16[16,9,512]{2,0,1:T(8,128)(2,1)S(1)}, bf16[16,9,512]{2,0,1:T(8,128)(2,1)S(1)}, u32[]{:S(2)}, u32[]{:S(2)}) %collective-permute-start.13) | collective-permute-done | bytes 147488 | tf_op jit(solution)/shard_map/ppermute | solution.py:28
  299.3 6.0 %collective-permute-done.14 = bf16[16,9,512]{2,0,1:T(8,128)(2,1)S(1)} collective-permute-done((bf16[16,9,512]{2,0,1:T(8,128)(2,1)S(1)}, bf16[16,9,512]{2,0,1:T(8,128)(2,1)S(1)}, u32[]{:S(2)}, u32[]{:S(2)}) %collective-permute-start.14) | collective-permute-done | bytes 147488 | tf_op jit(solution)/shard_map/ppermute | solution.py:28
  305.7 1.1 constant_dynamic-slice_fusion
  306.8 16.4 %all-gather.4.cloned.1.call-done = bf16[128,9,512]{2,0,1:T(8,128)(2,1)} async-done(((bf16[16,9,512]{2,0,1:T(8,128)(2,1)}), bf16[128,9,512]{2,0,1:T(8,128)(2,1)}) %all-gather.4.cloned.1.call-update) | async-done | bytes 1179664 | tf_op jit(solution)/shard_map/all_gather | solution.py:120
  323.3 6.2 %fusion.87 = (bf16[4,4,90,512]{3,2,1,0:T(8,128)(2,1)}, bf16[4,4,90,512]{3,2,1,0:T(8,128)(2,1)}, bf16[4,4,90,512]{3,2,1,0:T(8,128)(2,1)}, bf16[4,4,90,512]{3,2,1,...) fusion(bf16[4,6,92,512]{3,2,1,0:T(8,128)(2,1)S(1)} %get-tuple-e, ...), kind=kLoop, calls=%fused_computation.98 | loop fusion | bytes 26542080 | tf_op jit(solution)/shard_map/slice | solution.py:69
  329.5 2.6 reshape.74
  332.1 1.3 reshape.73
  333.4 1.3 reshape.72
  334.8 2.7 reshape.71
  337.4 1.3 reshape.70
  338.7 1.3 reshape.69
  340.1 2.6 reshape.68
  342.6 2.4 reshape.67
  345.5 36.1 %all-gather.8.cloned.1.call-done = bf16[512,9,512]{2,0,1:T(8,128)(2,1)} async-done(((bf16[128,9,512]{2,0,1:T(8,128)(2,1)}), bf16[512,9,512]{2,0,1:T(8,128)(2,1)}) %all-gather.8.cloned.1.call-update) | async-done | bytes 4718608 | tf_op jit(solution)/shard_map/all_gather | solution.py:144
  381.6 58.7 %all-gather.6.cloned.1.call-done = bf16[512,9,512]{2,0,1:T(8,128)(2,1)} async-done(((bf16[128,9,512]{2,0,1:T(8,128)(2,1)}), bf16[512,9,512]{2,0,1:T(8,128)(2,1)}) %all-gather.6.cloned.1.call-update) | async-done | bytes 4718608 | tf_op jit(solution)/shard_map/all_gather | solution.py:121
  440.2 2.2 fusion.73
  453.8 2.3 copy.42
  456.0 4.8 %copy.104 = bf16[512,9,512]{2,0,1:T(8,128)(2,1)} copy(bf16[512,9,512]{2,0,1:T(8,128)(2,1)} %all-gather.8.cloned.1.call-done) | data formatting | bytes 9437184
  (104 shorter events, 20.0 us)
Async XLA Ops:
  7.2 7.0 %copy-start.5 = (bf16[4,4,90,512]{3,1,2,0:T(4,128)(2,1)S(1)}, bf16[4,4,90,512]{3,1,2,0:T(4,128)(2,1)}, u32[]{:S(2)}) copy-start(bf16[4,4,90,512]{3,1,2,0:T(4,128)(2,1)} %param.5) | copy-start | bytes 4423684
  7.2 171.8 %reduce-scatter.3.cloned.1.call-start = ((), (), s32[]{:S(2)}) async-start(), calls=%async_computation.4 | async-start | bytes 11796480 | tf_op jit(solution)/shard_map/reduce_scatter | solution.py:124
  11.2 14.2 %collective-permute-start = (bf16[4,1,90,512]{3,2,1,0:T(8,128)(2,1)}, bf16[4,1,90,512]{3,2,1,0:T(8,128)(2,1)}, u32[]{:S(2)}, u32[]{:S(2)}) collective-permute-start(bf16[4,1,90,512]{3,2,1,0:T(8,128)(2,1)} %copy.72), channel_id=1, source_target_pairs={{0,8},{8,16},{16,24},{24,0},{1,9},{9,17},{17,25},{25,1},{2,10},{10... | collective-permute-start | bytes 1105928 | tf_op jit(solution)/shard_map/ppermute | solution.py:44
  15.2 11.2 %copy-start.6 = (bf16[4,4,90,512]{3,1,2,0:T(4,128)(2,1)S(1)}, bf16[4,4,90,512]{3,1,2,0:T(4,128)(2,1)}, u32[]{:S(2)}) copy-start(bf16[4,4,90,512]{3,1,2,0:T(4,128)(2,1)} %param.6) | copy-start | bytes 4423684
  16.1 38.8 %collective-permute-start.4 = (bf16[4,1,90,512]{3,2,1,0:T(8,128)(2,1)}, bf16[4,1,90,512]{3,2,1,0:T(8,128)(2,1)}, u32[]{:S(2)}, u32[]{:S(2)}) collective-permute-start(bf16[4,1,90,512]{3,2,1,0:T(8,128)(2,1)} %copy.74), channel_id=1, source_target_pairs={{0,8},{8,16},{16,24},{24,0},{1,9},{9,17},{17,25},{25,1},{2,10},{10... | collective-permute-start | bytes 1105928 | tf_op jit(solution)/shard_map/ppermute | solution.py:44
  17.6 38.6 %collective-permute-start.5 = (bf16[4,1,90,512]{3,2,1,0:T(8,128)(2,1)S(1)}, bf16[4,1,90,512]{3,2,1,0:T(8,128)(2,1)}, u32[]{:S(2)}, u32[]{:S(2)}) collective-permute-start(bf16[4,1,90,512]{3,2,1,0:T(8,128)(2,1)S(1)} %copy.75), channel_id=1, source_target_pairs={{8,0},{16,8},{24,16},{0,24},{9,1},{17,9},{25,17},{1,25},{10,2},{18... | collective-permute-start | bytes 1105928 | tf_op jit(solution)/shard_map/ppermute | solution.py:47
  19.9 30.2 %collective-permute-start.1 = (bf16[4,1,90,512]{3,2,1,0:T(8,128)(2,1)}, bf16[4,1,90,512]{3,2,1,0:T(8,128)(2,1)}, u32[]{:S(2)}, u32[]{:S(2)}) collective-permute-start(bf16[4,1,90,512]{3,2,1,0:T(8,128)(2,1)} %copy.73), channel_id=1, source_target_pairs={{8,0},{16,8},{24,16},{0,24},{9,1},{17,9},{25,17},{1,25},{10,2},{18... | collective-permute-start | bytes 1105928 | tf_op jit(solution)/shard_map/ppermute | solution.py:47
  51.2 9.7 %collective-permute-start.2 = (bf16[4,6,1,512]{3,2,1,0:T(2,128)(2,1)S(1)}, bf16[4,6,1,512]{3,2,1,0:T(2,128)(2,1)S(1)}, u32[]{:S(2)}, u32[]{:S(2)}) collective-permute-start(bf16[4,6,1,512]{3,2,1,0:T(2,128)(2,1)S(1)} %get-tuple-element.34), channel_id=1, source_target_pairs={{0,1},{1,2},{2,3},{3,4},{4,5},{5,6},{6,7},{7,0},{8,9},{9,10},{10,1... | collective-permute-start | bytes 73736 | tf_op jit(solution)/shard_map/ppermute | solution.py:44
  51.3 9.6 %collective-permute-start.3 = (bf16[4,6,1,512]{3,2,1,0:T(2,128)(2,1)S(1)}, bf16[4,6,1,512]{3,2,1,0:T(2,128)(2,1)S(1)}, u32[]{:S(2)}, u32[]{:S(2)}) collective-permute-start(bf16[4,6,1,512]{3,2,1,0:T(2,128)(2,1)S(1)} %get-tuple-element.35), channel_id=1, source_target_pairs={{1,0},{2,1},{3,2},{4,3},{5,4},{6,5},{7,6},{0,7},{9,8},{10,9},{11,1... | collective-permute-start | bytes 73736 | tf_op jit(solution)/shard_map/ppermute | solution.py:47
  57.3 5.6 %collective-permute-start.6 = (bf16[4,6,1,512]{3,2,1,0:T(2,128)(2,1)S(1)}, bf16[4,6,1,512]{3,2,1,0:T(2,128)(2,1)S(1)}, u32[]{:S(2)}, u32[]{:S(2)}) collective-permute-start(bf16[4,6,1,512]{3,2,1,0:T(2,128)(2,1)S(1)} %get-tuple-element.23), channel_id=1, source_target_pairs={{0,1},{1,2},{2,3},{3,4},{4,5},{5,6},{6,7},{7,0},{8,9},{9,10},{10,1... | collective-permute-start | bytes 73736 | tf_op jit(solution)/shard_map/ppermute | solution.py:44
  57.4 5.5 %collective-permute-start.7 = (bf16[4,6,1,512]{3,2,1,0:T(2,128)(2,1)S(1)}, bf16[4,6,1,512]{3,2,1,0:T(2,128)(2,1)S(1)}, u32[]{:S(2)}, u32[]{:S(2)}) collective-permute-start(bf16[4,6,1,512]{3,2,1,0:T(2,128)(2,1)S(1)} %get-tuple-element.24), channel_id=1, source_target_pairs={{1,0},{2,1},{3,2},{4,3},{5,4},{6,5},{7,6},{0,7},{9,8},{10,9},{11,1... | collective-permute-start | bytes 73736 | tf_op jit(solution)/shard_map/ppermute | solution.py:47
  60.9 4.7 copy-start.7
  83.8 174.8 %copy-start.17 = (f32[16,9,512]{2,0,1:T(8,128)S(1)}, f32[16,9,512]{2,0,1:T(8,128)}, u32[]{:S(2)}) copy-start(f32[16,9,512]{2,0,1:T(8,128)} %param.7) | copy-start | bytes 884740
  83.8 174.8 %copy-start.18 = (f32[16,9,512]{2,0,1:T(8,128)S(1)}, f32[16,9,512]{2,0,1:T(8,128)}, u32[]{:S(2)}) copy-start(f32[16,9,512]{2,0,1:T(8,128)} %param.8) | copy-start | bytes 884740
  83.8 174.8 %copy-start.19 = (f32[16,9,512]{2,0,1:T(8,128)S(1)}, f32[16,9,512]{2,0,1:T(8,128)}, u32[]{:S(2)}) copy-start(f32[16,9,512]{2,0,1:T(8,128)} %param.9) | copy-start | bytes 884740
  83.9 134.4 %reduce-scatter.5.cloned.1.call-start = ((), (), s32[]{:S(2)}) async-start(), calls=%async_computation.5 | async-start | bytes 2654208 | tf_op jit(solution)/shard_map/reduce_scatter | solution.py:130
  179.0 144.3 %all-gather.4.cloned.1.call-start = ((), (), s32[]{:S(2)}) async-start(), calls=%async_computation.2 | async-start | bytes 1327104 | tf_op jit(solution)/shard_map/all_gather | solution.py:120
  260.8 6.4 %collective-permute-start.8 = (bf16[16,9,512]{2,0,1:T(8,128)(2,1)S(1)}, bf16[16,9,512]{2,0,1:T(8,128)(2,1)S(1)}, u32[]{:S(2)}, u32[]{:S(2)}) collective-permute-start(bf16[16,9,512]{2,0,1:T(8,128)(2,1)S(1)} %get-tuple-element.18), channel_id=1, source_target_pairs={{0,1},{1,2},{2,3},{3,4},{4,5},{5,6},{6,7},{7,0},{8,9},{9,10},{10,1... | collective-permute-start | bytes 442376 | tf_op jit(solution)/shard_map/ppermute | solution.py:28
  267.1 6.4 %collective-permute-start.9 = (bf16[16,9,512]{2,0,1:T(8,128)(2,1)S(1)}, bf16[16,9,512]{2,0,1:T(8,128)(2,1)S(1)}, u32[]{:S(2)}, u32[]{:S(2)}) collective-permute-start(bf16[16,9,512]{2,0,1:T(8,128)(2,1)S(1)} %collective-permute-done.8), channel_id=1, source_target_pairs={{0,1},{1,2},{2,3},{3,4},{4,5},{5,6},{6,7},{7,0},{8,9},{9,10},{10,1... | collective-permute-start | bytes 442376 | tf_op jit(solution)/shard_map/ppermute | solution.py:28
  273.5 6.4 %collective-permute-start.10 = (bf16[16,9,512]{2,0,1:T(8,128)(2,1)S(1)}, bf16[16,9,512]{2,0,1:T(8,128)(2,1)S(1)}, u32[]{:S(2)}, u32[]{:S(2)}) collective-permute-start(bf16[16,9,512]{2,0,1:T(8,128)(2,1)S(1)} %collective-permute-done.9), channel_id=1, source_target_pairs={{0,1},{1,2},{2,3},{3,4},{4,5},{5,6},{6,7},{7,0},{8,9},{9,10},{10,1... | collective-permute-start | bytes 442376 | tf_op jit(solution)/shard_map/ppermute | solution.py:28
  279.9 6.4 %collective-permute-start.11 = (bf16[16,9,512]{2,0,1:T(8,128)(2,1)S(1)}, bf16[16,9,512]{2,0,1:T(8,128)(2,1)S(1)}, u32[]{:S(2)}, u32[]{:S(2)}) collective-permute-start(bf16[16,9,512]{2,0,1:T(8,128)(2,1)S(1)} %collective-permute-done.10), channel_id=1, source_target_pairs={{0,1},{1,2},{2,3},{3,4},{4,5},{5,6},{6,7},{7,0},{8,9},{9,10},{10,1... | collective-permute-start | bytes 442376 | tf_op jit(solution)/shard_map/ppermute | solution.py:28
  286.2 6.4 %collective-permute-start.12 = (bf16[16,9,512]{2,0,1:T(8,128)(2,1)S(1)}, bf16[16,9,512]{2,0,1:T(8,128)(2,1)S(1)}, u32[]{:S(2)}, u32[]{:S(2)}) collective-permute-start(bf16[16,9,512]{2,0,1:T(8,128)(2,1)S(1)} %collective-permute-done.11), channel_id=1, source_target_pairs={{0,1},{1,2},{2,3},{3,4},{4,5},{5,6},{6,7},{7,0},{8,9},{9,10},{10,1... | collective-permute-start | bytes 442376 | tf_op jit(solution)/shard_map/ppermute | solution.py:28
  292.6 6.4 %collective-permute-start.13 = (bf16[16,9,512]{2,0,1:T(8,128)(2,1)S(1)}, bf16[16,9,512]{2,0,1:T(8,128)(2,1)S(1)}, u32[]{:S(2)}, u32[]{:S(2)}) collective-permute-start(bf16[16,9,512]{2,0,1:T(8,128)(2,1)S(1)} %collective-permute-done.12), channel_id=1, source_target_pairs={{0,1},{1,2},{2,3},{3,4},{4,5},{5,6},{6,7},{7,0},{8,9},{9,10},{10,1... | collective-permute-start | bytes 442376 | tf_op jit(solution)/shard_map/ppermute | solution.py:28
  299.0 6.4 %collective-permute-start.14 = (bf16[16,9,512]{2,0,1:T(8,128)(2,1)S(1)}, bf16[16,9,512]{2,0,1:T(8,128)(2,1)S(1)}, u32[]{:S(2)}, u32[]{:S(2)}) collective-permute-start(bf16[16,9,512]{2,0,1:T(8,128)(2,1)S(1)} %collective-permute-done.13), channel_id=1, source_target_pairs={{0,1},{1,2},{2,3},{3,4},{4,5},{5,6},{6,7},{7,0},{8,9},{9,10},{10,1... | collective-permute-start | bytes 442376 | tf_op jit(solution)/shard_map/ppermute | solution.py:28
  299.0 82.5 %all-gather.8.cloned.1.call-start = ((), (), s32[]{:S(2)}) async-start(), calls=%async_computation.6 | async-start | bytes 5898240 | tf_op jit(solution)/shard_map/all_gather | solution.py:144
  306.8 133.4 %all-gather.6.cloned.1.call-start = ((), (), s32[]{:S(2)}) async-start(), calls=%async_computation.3 | async-start | bytes 5898240 | tf_op jit(solution)/shard_map/all_gather | solution.py:121
  329.5 2.6 copy-start.4
  329.5 4.0 copy-start.3
  333.4 4.0 copy-start.2
  334.8 4.0 copy-start.1
  340.1 5.0 %copy-start = (bf16[4,4,90,512]{3,2,1,0:T(8,128)(2,1)S(1)}, bf16[4,4,90,512]{3,2,1,0:T(8,128)(2,1)}, u32[]{:S(2)}) copy-start(bf16[4,4,90,512]{3,2,1,0:T(8,128)(2,1)} %get-tuple-element.33) | copy-start | bytes 4423684
  345.5 96.9 %copy-start.15 = (bf16[1440,512]{1,0:T(8,128)(2,1)S(1)}, bf16[1440,512]{1,0:T(8,128)(2,1)}, u32[]{:S(2)}) copy-start(bf16[1440,512]{1,0:T(8,128)(2,1)} %reshape.67) | copy-start | bytes 4423684
  440.2 2.5 copy-start.16
  442.7 1.4 copy-start.14
  444.1 1.4 copy-start.13
  445.5 1.4 copy-start.12
  446.8 1.4 copy-start.11
  448.2 1.4 copy-start.10
  449.6 1.4 copy-start.9
  451.0 1.4 copy-start.8
Sparse Core Ops, SparseCore 0:
  83.9 94.9 reduce-scatter.2
  181.3 36.9 reduce-scatter.4
  299.1 24.0 all-gather.3
  324.9 56.5 all-gather.7
  383.3 56.9 all-gather.5
